TPU v7x, 32 devices: a whole 2x2x4 slice. The times are simulated.
32 devices in a mesh: pipe: 2 (over x), dp: 8 (over z, y), tensor: 2 (over core).
Axes of the slice: x: 2, y: 2, z: 4, core: 2. Of those that a mesh axis runs over, the one named last changes fastest.
Arguments:
- inputs: bfloat16 [2, 8, 256, 1536], P(None, 'dp'), may hold values from -6 to 6
- cotangents: bfloat16 [2, 8, 256, 1536], P(None, 'dp'), may hold values from -6 to 6
- norm_scales: float32 [2, 1536, 2], P('pipe'), may hold values from 0.5 to 1.5
- w_query: bfloat16 [2, 1536, 1536], P('pipe', None, 'tensor'), may hold values from -0.15625 to 0.15625
- key_weight: bfloat16 [2, 1536, 768], P('pipe', None, 'tensor'), may hold values from -0.15625 to 0.15625
- value_weight: bfloat16 [2, 1536, 768], P('pipe', None, 'tensor'), may hold values from -0.15625 to 0.15625
- w_out: bfloat16 [2, 1536, 1536], P('pipe', None, 'tensor'), may hold values from -0.875 to 0.875
- w_gate: bfloat16 [2, 1536, 4096], P('pipe', None, 'tensor'), may hold values from -0.15625 to 0.15625
- w_up: bfloat16 [2, 1536, 4096], P('pipe', None, 'tensor'), may hold values from -0.15625 to 0.15625
- down_weight: bfloat16 [2, 1536, 4096], P('pipe', None, 'tensor'), may hold values from -0.09375 to 0.09375
Outputs:
- section_out: bfloat16 [2, 2, 8, 256, 1536], P('pipe', None, 'dp')
- section_in_grad: bfloat16 [2, 2, 8, 256, 1536], P('pipe', None, 'dp')
- grad_scales: float32 [2, 1536, 2], P('pipe', 'dp')
- grad_query: float32 [2, 1536, 1536], P('pipe', 'dp', 'tensor')
- grad_key: float32 [2, 1536, 768], P('pipe', 'dp', 'tensor')
- value_weight_gradient: float32 [2, 1536, 768], P('pipe', 'dp', 'tensor')
- grad_out: float32 [2, 1536, 1536], P('pipe', 'dp', 'tensor')
- grad_gate: float32 [2, 1536, 4096], P('pipe', 'dp', 'tensor')
- grad_up: float32 [2, 1536, 4096], P('pipe', 'dp', 'tensor')
- grad_down: float32 [2, 1536, 4096], P('pipe', 'dp', 'tensor')
All inputs are finite; a program needn't handle non-finite values.
Results may differ from a plain program's by a relative error of at most 0.03.
Values may be sent and summed in bfloat16 or wider, within the bound.
A program may use at most 256 MiB of HBM per device.

v0:
```python
import jax
import jax.numpy as jnp
from jax import lax
from jax.sharding import PartitionSpec as P

HEAD_SIZE = 96
EPS = 1e-05
THETA = 100000.0


def passed_along(value, axis, by):
    peers = lax.axis_size(axis)
    pairs = [(i, i + by) for i in range(peers) if 0 <= i + by < peers]
    return lax.ppermute(value, axis, pairs)


def rope_tables(length, size):
    positions = jnp.arange(length, dtype=jnp.float32)
    freqs = THETA ** (-(jnp.arange(size // 2, dtype=jnp.float32) * 2.0 / size))
    angles = positions[:, None] * freqs[None, :]
    cosine = jnp.concatenate([jnp.cos(angles), jnp.cos(angles)], axis=-1)
    sine = jnp.concatenate([jnp.sin(angles), jnp.sin(angles)], axis=-1)
    return (cosine[:, None, :], sine[:, None, :])


def rotate(values, cosine, sine):
    half = values.shape[-1] // 2
    turned = jnp.concatenate([-values[..., half:], values[..., :half]], axis=-1)
    return values * cosine + turned * sine


def rotate_back(grads, cosine, sine):
    half = grads.shape[-1] // 2
    moved = grads * sine
    turned = jnp.concatenate([moved[..., half:], -moved[..., :half]], axis=-1)
    return grads * cosine + turned


def times_t(left, right):
    return lax.dot_general(
        left, right, (((1,), (1,)), ((), ())), preferred_element_type=jnp.float32
    )


def over_rows(left, right):
    return lax.dot_general(
        left, right, (((0,), (0,)), ((), ())), preferred_element_type=jnp.float32
    )


def heads_total(partial_value):
    return lax.psum(partial_value.astype(jnp.bfloat16), "tensor").astype(jnp.float32)


def inputs_total(partial_value):
    return lax.psum(partial_value.astype(jnp.bfloat16), "tensor").astype(jnp.float32)


def norm_rows(values, gain):
    scale = lax.rsqrt(jnp.mean(values * values, axis=-1, keepdims=True) + EPS)
    return (scale, (values * scale * gain).astype(jnp.bfloat16))


def score_table(query, keys):
    length = query.shape[0]
    scores = jnp.einsum(
        "qgrd,kgd->grqk", query, keys, preferred_element_type=jnp.float32
    ) * HEAD_SIZE ** (-0.5)
    causal = jnp.arange(length)[:, None] >= jnp.arange(length)[None, :]
    return (scores, causal)


def forward_layer(hidden, params):
    scales, w_query, key_weight, value_weight, w_out, w_gate, w_up, down_weight = params
    length = hidden.shape[0]
    groups = key_weight.shape[1] // HEAD_SIZE
    wide = hidden.astype(jnp.float32)
    scale_one, normed_one = norm_rows(wide, scales[:, 0])
    cosine, sine = rope_tables(length, HEAD_SIZE)
    query = (
        rotate(
            jnp.dot(normed_one, w_query, preferred_element_type=jnp.float32).reshape(
                length, -1, HEAD_SIZE
            ),
            cosine,
            sine,
        )
        .astype(jnp.bfloat16)
        .reshape(length, groups, -1, HEAD_SIZE)
    )
    keys = rotate(
        jnp.dot(normed_one, key_weight, preferred_element_type=jnp.float32).reshape(
            length, groups, HEAD_SIZE
        ),
        cosine,
        sine,
    ).astype(jnp.bfloat16)
    values = (
        jnp.dot(normed_one, value_weight, preferred_element_type=jnp.float32)
        .astype(jnp.bfloat16)
        .reshape(length, groups, HEAD_SIZE)
    )
    scores, causal = score_table(query, keys)
    log_total = jnp.log(jnp.sum(jnp.where(causal, jnp.exp(scores), 0.0), axis=-1))
    probs = jnp.where(causal, jnp.exp(scores - log_total[..., None]), 0.0).astype(jnp.bfloat16)
    mixed = (
        jnp.einsum("grqk,kgd->qgrd", probs, values, preferred_element_type=jnp.float32)
        .astype(jnp.bfloat16)
        .reshape(length, -1)
    )
    middle = wide + heads_total(times_t(mixed, w_out))
    scale_two, normed_two = norm_rows(middle, scales[:, 1])
    gate = jnp.dot(normed_two, w_gate, preferred_element_type=jnp.float32)
    upward = jnp.dot(normed_two, w_up, preferred_element_type=jnp.float32)
    activated = (gate * jax.nn.sigmoid(gate) * upward).astype(jnp.bfloat16)
    result = (middle + heads_total(times_t(activated, down_weight))).astype(jnp.bfloat16)
    record = (
        hidden,
        scale_one,
        normed_one,
        query,
        keys,
        values,
        mixed,
        log_total,
        middle,
        scale_two,
        normed_two,
        gate,
        upward,
        activated,
    )
    return (record, result)


def backward_feedforward(record, cotangent, params):
    (
        hidden,
        scale_one,
        normed_one,
        query,
        keys,
        values,
        mixed,
        log_total,
        middle,
        scale_two,
        normed_two,
        gate,
        upward,
        activated,
    ) = record
    scales, w_query, key_weight, value_weight, w_out, w_gate, w_up, down_weight = params
    grad_down = over_rows(cotangent, activated)
    d_act = jnp.dot(cotangent, down_weight, preferred_element_type=jnp.float32)
    sig = jax.nn.sigmoid(gate)
    d_gate = (d_act * upward * sig * (1.0 + gate * (1.0 - sig))).astype(jnp.bfloat16)
    d_up = (d_act * gate * sig).astype(jnp.bfloat16)
    grad_gate = over_rows(normed_two, d_gate)
    grad_up = over_rows(normed_two, d_up)
    d_normed = inputs_total(times_t(d_gate, w_gate) + times_t(d_up, w_up))
    weighted = d_normed * scales[:, 1]
    gain_two = jnp.sum(d_normed * middle * scale_two, axis=0)
    d_middle = (
        cotangent.astype(jnp.float32)
        + scale_two * weighted
        - middle * scale_two**3 * jnp.mean(weighted * middle, axis=-1, keepdims=True)
    )
    return (d_middle, (grad_gate, grad_up, grad_down, gain_two))


def backward_attention(record, d_middle, params):
    (
        hidden,
        scale_one,
        normed_one,
        query,
        keys,
        values,
        mixed,
        log_total,
        middle,
        scale_two,
        normed_two,
        gate,
        upward,
        activated,
    ) = record
    scales, w_query, key_weight, value_weight, w_out, w_gate, w_up, down_weight = params
    length = hidden.shape[0]
    groups = keys.shape[1]
    d_mid_low = d_middle.astype(jnp.bfloat16)
    grad_out = over_rows(d_mid_low, mixed)
    d_mixed = jnp.dot(d_mid_low, w_out, preferred_element_type=jnp.float32).astype(jnp.bfloat16)
    d_heads = d_mixed.reshape(length, groups, -1, HEAD_SIZE)
    scores, causal = score_table(query, keys)
    probs = jnp.where(causal, jnp.exp(scores - log_total[..., None]), 0.0)
    d_probs = jnp.einsum("qgrd,kgd->grqk", d_heads, values, preferred_element_type=jnp.float32)
    d_values = jnp.einsum(
        "grqk,qgrd->kgd", probs.astype(jnp.bfloat16), d_heads, preferred_element_type=jnp.float32
    )
    delta = jnp.sum(
        d_heads.astype(jnp.float32)
        * mixed.reshape(length, groups, -1, HEAD_SIZE).astype(jnp.float32),
        axis=-1,
    )
    d_scores = (
        probs * (d_probs - jnp.transpose(delta, (1, 2, 0))[..., None]) * HEAD_SIZE ** (-0.5)
    ).astype(jnp.bfloat16)
    cosine, sine = rope_tables(length, HEAD_SIZE)
    d_query = (
        rotate_back(
            jnp.einsum(
                "grqk,kgd->qgrd", d_scores, keys, preferred_element_type=jnp.float32
            ).reshape(length, -1, HEAD_SIZE),
            cosine,
            sine,
        )
        .astype(jnp.bfloat16)
        .reshape(length, -1)
    )
    d_keys = (
        rotate_back(
            jnp.einsum("grqk,qgrd->kgd", d_scores, query, preferred_element_type=jnp.float32),
            cosine,
            sine,
        )
        .astype(jnp.bfloat16)
        .reshape(length, -1)
    )
    d_vals = d_values.astype(jnp.bfloat16).reshape(length, -1)
    grad_query = over_rows(normed_one, d_query)
    grad_key = over_rows(normed_one, d_keys)
    value_weight_gradient = over_rows(normed_one, d_vals)
    d_first = inputs_total(
        times_t(d_query, w_query) + times_t(d_keys, key_weight) + times_t(d_vals, value_weight)
    )
    weighted_one = d_first * scales[:, 0]
    wide = hidden.astype(jnp.float32)
    gain_one = jnp.sum(d_first * wide * scale_one, axis=0)
    d_hidden = (
        d_middle
        + scale_one * weighted_one
        - wide * scale_one**3 * jnp.mean(weighted_one * wide, axis=-1, keepdims=True)
    ).astype(jnp.bfloat16)
    return (d_hidden, (grad_query, grad_key, value_weight_gradient, grad_out, gain_one))


def body(
    inputs,
    cotangents,
    norm_scales,
    w_query,
    key_weight,
    value_weight,
    w_out,
    w_gate,
    w_up,
    down_weight,
):
    params = (
        norm_scales[0],
        w_query[0],
        key_weight[0],
        value_weight[0],
        w_out[0],
        w_gate[0],
        w_up[0],
        down_weight[0],
    )
    section_index = lax.axis_index("pipe")
    is_first = section_index == 0
    micros = inputs.shape[0]
    length = inputs.shape[2]
    width = inputs.shape[3]
    incoming = jnp.zeros((length, width), jnp.bfloat16)
    saved = []
    results = []
    for step_index in range(micros + 1):
        own_input = inputs[min(step_index, micros - 1), 0]
        record, result = forward_layer(jnp.where(is_first, own_input, incoming), params)
        saved.append(record)
        results.append(result)
        if step_index < micros:
            incoming = passed_along(result, "pipe", 1)
    stacked = jax.tree.map(lambda *entries: jnp.stack(entries), *saved)
    returned = jnp.zeros((length, width), jnp.bfloat16)
    in_grads = []
    for step_index in range(micros + 1):
        micro_index = step_index - 1 + section_index
        weight_mask = jnp.logical_and(micro_index >= 0, micro_index < micros).astype(jnp.float32)
        slot_index = jnp.clip(micro_index + section_index, 0, micros)
        record = jax.tree.map(
            lambda entry: lax.dynamic_index_in_dim(entry, slot_index, 0, keepdims=False), stacked
        )
        cotangent = jnp.where(is_first, returned, cotangents[min(step_index, micros - 1), 0])
        d_middle, ffn_part = backward_feedforward(record, cotangent, params)
        if step_index == 0:
            ffn_sums = jax.tree.map(lambda extra: weight_mask * extra, ffn_part)
        else:
            ffn_sums = jax.tree.map(
                lambda total, extra: total + weight_mask * extra, ffn_sums, ffn_part
            )
        d_hidden, attn_part = backward_attention(record, d_middle, params)
        if step_index == 0:
            attn_sums = jax.tree.map(lambda extra: weight_mask * extra, attn_part)
        else:
            attn_sums = jax.tree.map(
                lambda total, extra: total + weight_mask * extra, attn_sums, attn_part
            )
        in_grads.append(d_hidden)
        if step_index < micros:
            returned = passed_along(d_hidden, "pipe", -1)
    gain_grads = jnp.stack([attn_sums[4], ffn_sums[3]], axis=1)[None]
    shards = (
        lax.psum_scatter(
            attn_sums[0][None].astype(jnp.bfloat16), "dp", scatter_dimension=1, tiled=True
        ).astype(jnp.float32),
        lax.psum_scatter(
            attn_sums[1][None].astype(jnp.bfloat16), "dp", scatter_dimension=1, tiled=True
        ).astype(jnp.float32),
        lax.psum_scatter(
            attn_sums[2][None].astype(jnp.bfloat16), "dp", scatter_dimension=1, tiled=True
        ).astype(jnp.float32),
        lax.psum_scatter(
            attn_sums[3][None].astype(jnp.bfloat16), "dp", scatter_dimension=1, tiled=True
        ).astype(jnp.float32),
        lax.psum_scatter(
            ffn_sums[0][None].astype(jnp.bfloat16), "dp", scatter_dimension=1, tiled=True
        ).astype(jnp.float32),
        lax.psum_scatter(
            ffn_sums[1][None].astype(jnp.bfloat16), "dp", scatter_dimension=1, tiled=True
        ).astype(jnp.float32),
        lax.psum_scatter(
            ffn_sums[2][None].astype(jnp.bfloat16), "dp", scatter_dimension=1, tiled=True
        ).astype(jnp.float32),
        lax.psum_scatter(
            gain_grads.astype(jnp.bfloat16), "dp", scatter_dimension=1, tiled=True
        ).astype(jnp.float32),
    )
    (
        grad_query,
        grad_key,
        value_weight_gradient,
        grad_out,
        grad_gate,
        grad_up,
        grad_down,
        grad_scales,
    ) = shards
    section_out = lax.dynamic_slice_in_dim(jnp.stack(results), section_index, micros, 0).reshape(
        1, micros, 1, length, width
    )
    section_in_grad = lax.dynamic_slice_in_dim(
        jnp.stack(in_grads), 1 - section_index, micros, 0
    ).reshape(1, micros, 1, length, width)
    return (
        section_out,
        section_in_grad,
        grad_scales,
        grad_query,
        grad_key,
        value_weight_gradient,
        grad_out,
        grad_gate,
        grad_up,
        grad_down,
    )


def solution(mesh):
    placed = (
        P(None, "dp", None, None),
        P(None, "dp", None, None),
        P("pipe", None, None),
        P("pipe", None, "tensor"),
        P("pipe", None, "tensor"),
        P("pipe", None, "tensor"),
        P("pipe", None, "tensor"),
        P("pipe", None, "tensor"),
        P("pipe", None, "tensor"),
        P("pipe", None, "tensor"),
    )
    return jax.shard_map(
        body,
        mesh=mesh,
        in_specs=placed,
        out_specs=(
            P("pipe", None, "dp", None, None),
            P("pipe", None, "dp", None, None),
            P("pipe", "dp", None),
            P("pipe", "dp", "tensor"),
            P("pipe", "dp", "tensor"),
            P("pipe", "dp", "tensor"),
            P("pipe", "dp", "tensor"),
            P("pipe", "dp", "tensor"),
            P("pipe", "dp", "tensor"),
            P("pipe", "dp", "tensor"),
        ),
        check_vma=False,
    )
```

profile of v0, /device:TPU:0, one launch (start us, length us, event | category | flops | bytes accessed | tf_op | source)
XLA Modules:
  0.0 1268.2 jit_solution(18007858066272877327)
XLA Ops:
  13.6 4.3 copy.78
  17.9 2.8 fusion.323
  32.4 21.8 %all-reduce.13.cloned.1.call-done = bf16[256,1536]{1,0:T(8,128)(2,1)} async-done(((bf16[256,1536]{1,0:T(8,128)(2,1)}), bf16[256,1536]{1,0:T(8,128)(2,1)}) %all-reduce.13.cloned.1.call-update) | async-done | bytes 786448 | tf_op jit(solution)/shard_map/psum | solution.py:52
  56.1 2.8 fusion.216
  58.9 5.0 fusion.37
  64.0 3.5 multiply_convert_fusion.2
  68.5 2.7 fusion.70
  71.2 20.3 %all-reduce.15.cloned.1.call-done = bf16[256,1536]{1,0:T(8,128)(2,1)} async-done(((bf16[256,1536]{1,0:T(8,128)(2,1)}), bf16[256,1536]{1,0:T(8,128)(2,1)}) %all-reduce.15.cloned.1.call-update) | async-done | bytes 786448 | tf_op jit(solution)/shard_map/psum | solution.py:52
  93.4 4.4 collective-permute-start
  97.9 16.7 %collective-permute-done = bf16[256,1536]{1,0:T(8,128)(2,1)S(1)} collective-permute-done((bf16[256,1536]{1,0:T(8,128)(2,1)S(1)}, bf16[256,1536]{1,0:T(8,128)(2,1)S(1)}, u32[]{:S(2)}, u32[]{:S(2)}) %collective-permute-start) | collective-permute-done | bytes 786464 | tf_op jit(solution)/shard_map/ppermute | solution.py:14
  128.9 21.0 %all-reduce.17.cloned.1.call-done = bf16[256,1536]{1,0:T(8,128)(2,1)} async-done(((bf16[256,1536]{1,0:T(8,128)(2,1)}), bf16[256,1536]{1,0:T(8,128)(2,1)}) %all-reduce.17.cloned.1.call-update) | async-done | bytes 786448 | tf_op jit(solution)/shard_map/psum | solution.py:52
  152.9 5.4 fusion.35
  158.3 3.4 multiply_convert_fusion.1
  162.7 2.7 fusion.73
  165.5 20.3 %all-reduce.19.cloned.1.call-done = bf16[256,1536]{1,0:T(8,128)(2,1)} async-done(((bf16[256,1536]{1,0:T(8,128)(2,1)}), bf16[256,1536]{1,0:T(8,128)(2,1)}) %all-reduce.19.cloned.1.call-update) | async-done | bytes 786448 | tf_op jit(solution)/shard_map/psum | solution.py:52
  185.8 3.0 fusion.456
  188.8 4.6 collective-permute-start.1
  193.4 16.6 %collective-permute-done.1 = bf16[256,1536]{1,0:T(8,128)(2,1)} collective-permute-done((bf16[256,1536]{1,0:T(8,128)(2,1)}, bf16[256,1536]{1,0:T(8,128)(2,1)}, u32[]{:S(2)}, u32[]{:S(2)}) %collective-permute-start.1) | collective-permute-done | bytes 786464 | tf_op jit(solution)/shard_map/ppermute | solution.py:14
  235.1 11.6 all-reduce.21.cloned.1.call-done
  249.7 5.4 fusion.33
  255.1 3.2 multiply_convert_fusion
  263.1 7.5 fusion.132
  272.7 5.5 fusion.67
  279.1 4.8 pad_maximum_fusion.2
  283.9 14.7 %all-reduce.23.cloned.1.call-done = bf16[256,1536]{1,0:T(8,128)(2,1)} async-done(((bf16[256,1536]{1,0:T(8,128)(2,1)}), bf16[256,1536]{1,0:T(8,128)(2,1)}) %all-reduce.23.cloned.1.call-update) | async-done | bytes 786448 | tf_op jit(solution)/shard_map/psum | solution.py:56
  298.6 2.8 fusion.181
  324.6 16.6 %all-reduce.25.cloned.1.call-done = bf16[256,1536]{1,0:T(8,128)(2,1)} async-done(((bf16[256,1536]{1,0:T(8,128)(2,1)}), bf16[256,1536]{1,0:T(8,128)(2,1)}) %all-reduce.25.cloned.1.call-update) | async-done | bytes 786448 | tf_op jit(solution)/shard_map/psum | solution.py:56
  341.2 2.6 fusion.204
  347.8 20.0 %collective-permute-done.2 = bf16[256,1536]{1,0:T(8,128)(2,1)S(1)} collective-permute-done((bf16[256,1536]{1,0:T(8,128)(2,1)S(1)}, bf16[256,1536]{1,0:T(8,128)(2,1)S(1)}, u32[]{:S(2)}, u32[]{:S(2)}) %collective-permute-start.2) | collective-permute-done | bytes 786464 | tf_op jit(solution)/shard_map/ppermute | solution.py:14
  367.9 6.6 fusion.118
  376.7 2.7 fusion.64
  379.5 3.1 fusion.112
  382.6 16.1 %all-reduce.27.cloned.1.call-done = bf16[256,1536]{1,0:T(8,128)(2,1)} async-done(((bf16[256,1536]{1,0:T(8,128)(2,1)}), bf16[256,1536]{1,0:T(8,128)(2,1)}) %all-reduce.27.cloned.1.call-update) | async-done | bytes 786448 | tf_op jit(solution)/shard_map/psum | solution.py:56
  398.7 2.8 fusion.183
  422.3 18.9 %all-reduce.29.cloned.1.call-done = bf16[256,1536]{1,0:T(8,128)(2,1)} async-done(((bf16[256,1536]{1,0:T(8,128)(2,1)}), bf16[256,1536]{1,0:T(8,128)(2,1)}) %all-reduce.29.cloned.1.call-update) | async-done | bytes 786448 | tf_op jit(solution)/shard_map/psum | solution.py:56
  447.2 3.1 fusion.98
  450.3 17.2 %collective-permute-done.3 = bf16[256,1536]{1,0:T(8,128)(2,1)S(1)} collective-permute-done((bf16[256,1536]{1,0:T(8,128)(2,1)S(1)}, bf16[256,1536]{1,0:T(8,128)(2,1)S(1)}, u32[]{:S(2)}, u32[]{:S(2)}) %collective-permute-start.3) | collective-permute-done | bytes 786464 | tf_op jit(solution)/shard_map/ppermute | solution.py:14
  467.6 6.6 fusion.104
  474.3 5.4 fusion.15
  479.6 5.5 fusion.61
  486.7 5.8 fusion.76
  492.5 12.1 all-reduce.31.cloned.1.call-done
  504.6 2.8 fusion.185
  529.3 19.4 %all-reduce.33.cloned.1.call-done = (bf16[256,1536]{1,0:T(8,128)(2,1)}, bf16[256,1536]{1,0:T(8,128)(2,1)}) async-done(((bf16[256,1536]{1,0:T(8,128)(2,1)}, bf16[256,1536]{1,0:T(8,128)(2,1)}), (bf16[256,1536]{1,0:T(8,128)(2,1)}, bf16[256,1536]{1,0:T(8,128)(2,1)})) %all-reduce.33.cloned.1.call-update) | async-done | bytes 1572880 | tf_op jit(solution)/shard_map/psum | solution.py:52
  554.5 4.4 fusion.452
  572.1 2.7 fusion.44
  578.9 2.7 fusion.43
  584.5 6.4 fusion.300
  590.9 6.5 fusion.296
  597.4 12.5 fusion
  611.1 7.7 fusion.298
  618.8 6.5 fusion.294
  625.3 12.6 fusion.1
  641.2 6.4 fusion.258
  647.6 6.5 fusion.256
  654.2 12.6 fusion.2
  666.8 3.8 fusion.194
  674.1 11.2 reduce-scatter.13.cloned.1.call-done
  686.9 65.5 %reduce-scatter.15.cloned.1.call-done = bf16[1,192,384]{2,1,0:T(8,128)(2,1)} async-done(((bf16[1,1536,384]{2,1,0:T(8,128)(2,1)}), bf16[1,192,384]{2,1,0:T(8,128)(2,1)}) %reduce-scatter.15.cloned.1.call-update) | async-done | bytes 147472 | tf_op jit(solution)/shard_map/reduce_scatter | solution.py:322
  754.1 70.3 %reduce-scatter.17.cloned.1.call-done = bf16[1,192,768]{2,1,0:T(8,128)(2,1)} async-done(((bf16[1,1536,768]{2,1,0:T(8,128)(2,1)}), bf16[1,192,768]{2,1,0:T(8,128)(2,1)}) %reduce-scatter.17.cloned.1.call-update) | async-done | bytes 294928 | tf_op jit(solution)/shard_map/reduce_scatter | solution.py:325
  826.2 70.4 %reduce-scatter.11.cloned.1.call-done = bf16[1,192,768]{2,1,0:T(8,128)(2,1)} async-done(((bf16[1,1536,768]{2,1,0:T(8,128)(2,1)}), bf16[1,192,768]{2,1,0:T(8,128)(2,1)}) %reduce-scatter.11.cloned.1.call-update) | async-done | bytes 294928 | tf_op jit(solution)/shard_map/reduce_scatter | solution.py:316
  898.4 118.9 %reduce-scatter.19.cloned.1.call-done = bf16[1,192,2048]{2,1,0:T(8,128)(2,1)} async-done(((bf16[1,1536,2048]{2,1,0:T(8,128)(2,1)}), bf16[1,192,2048]{2,1,0:T(8,128)(2,1)}) %reduce-scatter.19.cloned.1.call-update) | async-done | bytes 786448 | tf_op jit(solution)/shard_map/reduce_scatter | solution.py:328
  1019.8 118.3 %reduce-scatter.21.cloned.1.call-done = bf16[1,192,2048]{2,1,0:T(8,128)(2,1)} async-done(((bf16[1,1536,2048]{2,1,0:T(8,128)(2,1)}), bf16[1,192,2048]{2,1,0:T(8,128)(2,1)}) %reduce-scatter.21.cloned.1.call-update) | async-done | bytes 786448 | tf_op jit(solution)/shard_map/reduce_scatter | solution.py:331
  1140.5 118.4 %reduce-scatter.23.cloned.1.call-done = bf16[1,192,2048]{2,1,0:T(8,128)(2,1)} async-done(((bf16[1,1536,2048]{2,1,0:T(8,128)(2,1)}), bf16[1,192,2048]{2,1,0:T(8,128)(2,1)}) %reduce-scatter.23.cloned.1.call-update) | async-done | bytes 786448 | tf_op jit(solution)/shard_map/reduce_scatter | solution.py:334
  (586 shorter events, 203.5 us)
Async XLA Ops:
  7.2 23.4 %copy-start = (bf16[1,1536,768]{2,1,0:T(8,128)(2,1)S(1)}, bf16[1,1536,768]{2,1,0:T(8,128)(2,1)}, u32[]{:S(2)}) copy-start(bf16[1,1536,768]{2,1,0:T(8,128)(2,1)} %param.16) | copy-start | bytes 7077892
  7.2 47.0 %all-reduce.13.cloned.1.call-start = ((), (), s32[]{:S(2)}) async-start(), calls=%async_computation.8 | async-start | bytes 1572864 | tf_op jit(solution)/shard_map/psum | solution.py:52
  10.7 7.3 copy-start.153
  32.3 59.2 %all-reduce.15.cloned.1.call-start = ((), (), s32[]{:S(2)}) async-start(), calls=%async_computation.9 | async-start | bytes 1572864 | tf_op jit(solution)/shard_map/psum | solution.py:52
  56.1 7.8 slice-start
  58.9 9.6 slice-start.10
  68.5 23.1 %copy-start.40 = (bf16[256,1536]{1,0:T(8,128)(2,1)S(1)}, bf16[256,1536]{1,0:T(8,128)(2,1)}, u32[]{:S(2)}) copy-start(bf16[256,1536]{1,0:T(8,128)(2,1)} %all-reduce.13.cloned.1.call-done) | copy-start | bytes 2359300
  71.2 78.7 %all-reduce.17.cloned.1.call-start = ((), (), s32[]{:S(2)}) async-start(), calls=%async_computation.10 | async-start | bytes 1572864 | tf_op jit(solution)/shard_map/psum | solution.py:52
  91.5 23.0 %copy-start.13 = (bf16[2,1,256,1536]{3,2,1,0:T(8,128)(2,1)S(1)}, bf16[2,1,256,1536]{3,2,1,0:T(8,128)(2,1)}, u32[]{:S(2)}) copy-start(bf16[2,1,256,1536]{3,2,1,0:T(8,128)(2,1)} %param.10) | copy-start | bytes 4718596
  91.5 23.4 %copy-start.24 = (bf16[1,1536,384]{2,1,0:T(8,128)(2,1)S(1)}, bf16[1,1536,384]{2,1,0:T(8,128)(2,1)}, u32[]{:S(2)}) copy-start(bf16[1,1536,384]{2,1,0:T(8,128)(2,1)} %param.15) | copy-start | bytes 3538948
  93.4 22.9 %copy-start.78 = (bf16[256,1536]{1,0:T(8,128)(2,1)}, bf16[256,1536]{1,0:T(8,128)(2,1)S(1)}, u32[]{:S(2)}) copy-start(bf16[256,1536]{1,0:T(8,128)(2,1)S(1)} %add_convert_fusion.7) | copy-start | bytes 2359300
  93.4 22.9 %copy-start.81 = (bf16[1,1536,768]{1,2,0:T(8,128)(2,1)S(1)}, bf16[1,1536,768]{1,2,0:T(8,128)(2,1)}, u32[]{:S(2)}) copy-start(bf16[1,1536,768]{1,2,0:T(8,128)(2,1)} %copy.78) | copy-start | bytes 7077892
  93.4 21.1 %collective-permute-start = (bf16[256,1536]{1,0:T(8,128)(2,1)S(1)}, bf16[256,1536]{1,0:T(8,128)(2,1)S(1)}, u32[]{:S(2)}, u32[]{:S(2)}) collective-permute-start(bf16[256,1536]{1,0:T(8,128)(2,1)S(1)} %add_convert_fusion.7), channel_id=1, source_target_pairs={{0,16},{1,17},{2,18},{3,19},{4,20},{5,21},{6,22},{7,23},{8,24},{9,... | collective-permute-start | bytes 2359304 | tf_op jit(solution)/shard_map/ppermute | solution.py:14
  114.9 70.9 %copy-start.18 = (bf16[256,1536]{1,0:T(8,128)(2,1)}, bf16[256,1536]{1,0:T(8,128)(2,1)S(1)}, u32[]{:S(2)}) copy-start(bf16[256,1536]{1,0:T(8,128)(2,1)S(1)} %get-tuple-element.29) | copy-start | bytes 2359300
  128.8 57.0 %all-reduce.19.cloned.1.call-start = ((), (), s32[]{:S(2)}) async-start(), calls=%async_computation.11 | async-start | bytes 1572864 | tf_op jit(solution)/shard_map/psum | solution.py:52
  151.4 6.8 slice-start.2
  152.9 5.4 slice-start.3
  152.9 9.9 slice-start.12
  165.5 81.2 %all-reduce.21.cloned.1.call-start = ((), (), s32[]{:S(2)}) async-start(), calls=%async_computation.12 | async-start | bytes 1572864 | tf_op jit(solution)/shard_map/psum | solution.py:52
  188.8 21.2 %collective-permute-start.1 = (bf16[256,1536]{1,0:T(8,128)(2,1)}, bf16[256,1536]{1,0:T(8,128)(2,1)}, u32[]{:S(2)}, u32[]{:S(2)}) collective-permute-start(bf16[256,1536]{1,0:T(8,128)(2,1)} %get-tuple-element.46), channel_id=1, source_target_pairs={{0,16},{1,17},{2,18},{3,19},{4,20},{5,21},{6,22},{7,23},{8,24},{9,... | collective-permute-start | bytes 2359304 | tf_op jit(solution)/shard_map/ppermute | solution.py:14
  193.4 18.1 %copy-start.25 = (bf16[1,1536,384]{2,1,0:T(8,128)(2,1)S(1)}, bf16[1,1536,384]{2,1,0:T(8,128)(2,1)}, u32[]{:S(2)}) copy-start(bf16[1,1536,384]{2,1,0:T(8,128)(2,1)} %param.15) | copy-start | bytes 3538948
  193.4 19.5 %copy-start.82 = (bf16[1,1536,768]{1,2,0:T(8,128)(2,1)S(1)}, bf16[1,1536,768]{1,2,0:T(8,128)(2,1)}, u32[]{:S(2)}) copy-start(bf16[1,1536,768]{1,2,0:T(8,128)(2,1)} %copy.78) | copy-start | bytes 7077892
  225.4 73.2 %all-reduce.23.cloned.1.call-start = ((), (), s32[]{:S(2)}) async-start(), calls=%async_computation.13 | async-start | bytes 1572864 | tf_op jit(solution)/shard_map/psum | solution.py:56
  248.2 6.8 slice-start.4
  249.7 5.4 slice-start.5
  263.1 7.5 copy-start.47
  272.7 5.8 copy-start.162
  272.7 5.8 copy-start.164
  278.2 63.0 %all-reduce.25.cloned.1.call-start = ((), (), s32[]{:S(2)}) async-start(), calls=%async_computation.14 | async-start | bytes 1572864 | tf_op jit(solution)/shard_map/psum | solution.py:56
  320.9 77.8 %all-reduce.27.cloned.1.call-start = ((), (), s32[]{:S(2)}) async-start(), calls=%async_computation.15 | async-start | bytes 1572864 | tf_op jit(solution)/shard_map/psum | solution.py:56
  343.8 24.1 %copy-start.43 = (bf16[2,1,256,1536]{3,2,1,0:T(8,128)(2,1)S(1)}, bf16[2,1,256,1536]{3,2,1,0:T(8,128)(2,1)}, u32[]{:S(2)}) copy-start(bf16[2,1,256,1536]{3,2,1,0:T(8,128)(2,1)} %param.11) | copy-start | bytes 4718596
  343.8 30.8 %slice-start.6 = ((s8[6291456]{0:T(1024)(128)(4,1)}), s8[4194304]{0:T(1024)(128)(4,1)S(1)}, s32[]{:S(2)}) async-start(s8[6291456]{0:T(1024)(128)(4,1)} %bitcast.922), calls=%async_computation.33 | async-start | bytes 8388608
  343.8 32.8 %slice-start.8 = ((s8[6291456]{0:T(1024)(128)(4,1)}), s8[4194304]{0:T(1024)(128)(4,1)S(1)}, s32[]{:S(2)}) async-start(s8[6291456]{0:T(1024)(128)(4,1)} %bitcast.924), calls=%async_computation.35 | async-start | bytes 8388608
  345.8 22.0 %collective-permute-start.2 = (bf16[256,1536]{1,0:T(8,128)(2,1)S(1)}, bf16[256,1536]{1,0:T(8,128)(2,1)S(1)}, u32[]{:S(2)}, u32[]{:S(2)}) collective-permute-start(bf16[256,1536]{1,0:T(8,128)(2,1)S(1)} %fusion.176), channel_id=1, source_target_pairs={{16,0},{17,1},{18,2},{19,3},{20,4},{21,5},{22,6},{23,7},{24,8},{25... | collective-permute-start | bytes 2359304 | tf_op jit(solution)/shard_map/ppermute | solution.py:14
  367.9 6.7 copy-start.32
  367.9 6.7 slice-start.7
  367.9 8.7 slice-start.9
  379.4 61.9 %all-reduce.29.cloned.1.call-start = ((), (), s32[]{:S(2)}) async-start(), calls=%async_computation.16 | async-start | bytes 1572864 | tf_op jit(solution)/shard_map/psum | solution.py:56
  420.9 83.7 %all-reduce.31.cloned.1.call-start = ((), (), s32[]{:S(2)}) async-start(), calls=%async_computation.17 | async-start | bytes 1572864 | tf_op jit(solution)/shard_map/psum | solution.py:56
  445.8 21.7 %copy-start.44 = (bf16[2,1,256,1536]{3,2,1,0:T(8,128)(2,1)S(1)}, bf16[2,1,256,1536]{3,2,1,0:T(8,128)(2,1)}, u32[]{:S(2)}) copy-start(bf16[2,1,256,1536]{3,2,1,0:T(8,128)(2,1)} %param.11) | copy-start | bytes 4718596
  445.8 21.7 %collective-permute-start.3 = (bf16[256,1536]{1,0:T(8,128)(2,1)S(1)}, bf16[256,1536]{1,0:T(8,128)(2,1)S(1)}, u32[]{:S(2)}, u32[]{:S(2)}) collective-permute-start(bf16[256,1536]{1,0:T(8,128)(2,1)S(1)} %fusion.170), channel_id=1, source_target_pairs={{16,0},{17,1},{18,2},{19,3},{20,4},{21,5},{22,6},{23,7},{24,8},{25... | collective-permute-start | bytes 2359304 | tf_op jit(solution)/shard_map/ppermute | solution.py:14
  467.6 6.6 copy-start.37
  474.2 5.4 copy-start.119
  474.2 5.4 copy-start.121
  485.2 63.5 %all-reduce.33.cloned.1.call-start = ((), (), s32[]{:S(2)}) async-start(), calls=%async_computation.26 | async-start | bytes 3145728 | tf_op jit(solution)/shard_map/psum | solution.py:52
  526.9 23.7 %copy-start.146 = (f32[1536]{0:T(1024)S(1)}, f32[1536]{0:T(1024)}, u32[]{:S(2)}) copy-start(f32[1536]{0:T(1024)} %get-tuple-element.16) | copy-start | bytes 18436
  526.9 23.7 %copy-start.148 = (f32[1536]{0:T(1024)S(1)}, f32[1536]{0:T(1024)}, u32[]{:S(2)}) copy-start(f32[1536]{0:T(1024)} %get-tuple-element.18) | copy-start | bytes 18436
  526.9 145.7 %reduce-scatter.25.cloned.1.call-start = ((), (), s32[]{:S(2)}) async-start(), calls=%async_computation.25 | async-start | bytes 442368
  529.3 25.2 %copy-start.158 = (f32[256]{0:T(256)S(1)}, f32[256]{0:T(256)}, u32[]{:S(2)}) copy-start(f32[256]{0:T(256)} %copy-done.156) | copy-start | bytes 3076
  554.4 130.9 %reduce-scatter.13.cloned.1.call-start = ((), (), s32[]{:S(2)}) async-start(), calls=%async_computation.19 | async-start | bytes 1327104 | tf_op jit(solution)/shard_map/reduce_scatter | solution.py:319
  563.3 189.2 %reduce-scatter.15.cloned.1.call-start = ((), (), s32[]{:S(2)}) async-start(), calls=%async_computation.20 | async-start | bytes 1327104 | tf_op jit(solution)/shard_map/reduce_scatter | solution.py:322
  568.1 256.3 %reduce-scatter.17.cloned.1.call-start = ((), (), s32[]{:S(2)}) async-start(), calls=%async_computation.21 | async-start | bytes 2654208 | tf_op jit(solution)/shard_map/reduce_scatter | solution.py:325
  574.8 321.7 %reduce-scatter.11.cloned.1.call-start = ((), (), s32[]{:S(2)}) async-start(), calls=%async_computation.18 | async-start | bytes 2654208 | tf_op jit(solution)/shard_map/reduce_scatter | solution.py:316
  581.6 435.7 %reduce-scatter.19.cloned.1.call-start = ((), (), s32[]{:S(2)}) async-start(), calls=%async_computation.22 | async-start | bytes 7077888 | tf_op jit(solution)/shard_map/reduce_scatter | solution.py:328
  584.5 12.9 %copy-start.16 = (bf16[3,256,1536]{2,1,0:T(8,128)(2,1)}, bf16[3,256,1536]{2,1,0:T(8,128)(2,1)S(1)}, u32[]{:S(2)}) copy-start(bf16[3,256,1536]{2,1,0:T(8,128)(2,1)S(1)} %pad_maximum_fusion.6) | copy-start | bytes 7077892
  584.5 6.4 copy-start.118
  590.9 6.5 copy-start.122
  609.9 528.2 %reduce-scatter.21.cloned.1.call-start = ((), (), s32[]{:S(2)}) async-start(), calls=%async_computation.23 | async-start | bytes 7077888 | tf_op jit(solution)/shard_map/reduce_scatter | solution.py:331
  611.1 7.7 copy-start.17
  611.1 7.7 copy-start.116
  618.8 6.5 copy-start.120
  637.9 621.1 %reduce-scatter.23.cloned.1.call-start = ((), (), s32[]{:S(2)}) async-start(), calls=%async_computation.24 | async-start | bytes 7077888 | tf_op jit(solution)/shard_map/reduce_scatter | solution.py:334
  641.2 6.4 copy-start.34
  647.6 6.5 copy-start.39
  (142 other events, 336.1 us)
Sparse Core Ops, SparseCore 0:
  32.5 21.6 all-reduce.12
  71.3 20.1 all-reduce.14
  128.9 20.8 all-reduce.16
  165.6 20.1 all-reduce.18
  225.5 21.1 all-reduce.20
  278.4 20.1 all-reduce.22
  321.0 20.1 all-reduce.24
  379.5 19.1 all-reduce.26
  421.0 20.1 all-reduce.28
  485.3 19.2 all-reduce.30
  527.0 21.6 all-reduce.32
  554.5 63.3 reduce-scatter.24
  621.4 63.8 reduce-scatter.12
  688.5 63.8 reduce-scatter.14
  755.8 68.5 reduce-scatter.16
  827.7 68.8 reduce-scatter.10
  900.0 117.2 reduce-scatter.18
  1020.8 117.2 reduce-scatter.20
  1141.7 117.2 reduce-scatter.22
where the time goes:
time: 1280 us; the launch traced here: 1270 us
  waiting for transfers between devices  837 us (65%)
  matrix products  240 us (19%)
  other arithmetic  105 us (8%)
  local copies, waits for them, and re-layouts  55.1 us (4%)
  between operations  16.5 us (1%)
  starting transfers between devices  14.8 us (1%)
    reduce_scatter x1, waiting for transfers between devices, body(): lax.psum_scatter(ffn_sums[0][None].astype(jnp.bfloat16), 'dp', scatter_di...  119 us
    reduce_scatter x1, waiting for transfers between devices, body(): lax.psum_scatter(ffn_sums[2][None].astype(jnp.bfloat16), 'dp', scatter_di...  118 us
    reduce_scatter x1, waiting for transfers between devices, body(): lax.psum_scatter(ffn_sums[1][None].astype(jnp.bfloat16), 'dp', scatter_di...  118 us
    psum x6, waiting for transfers between devices, heads_total(): lax.psum(partial_value.astype(jnp.bfloat16), 'tensor').astype(jnp.float32)  114 us
    dot_general x21, matrix products, over_rows(): lax.dot_general(left, right, (((0,), (0,)), ((), ())), preferred_element_...  96.3 us
    psum x5, waiting for transfers between devices, inputs_total(): lax.psum(partial_value.astype(jnp.bfloat16), 'tensor').astype(jnp.float32)  78.4 us
    ppermute x4, waiting for transfers between devices, passed_along(): return lax.ppermute(value, axis, pairs)  70.5 us
    reduce_scatter x1, waiting for transfers between devices, body(): lax.psum_scatter(attn_sums[0][None].astype(jnp.bfloat16), 'dp', scatter_d...  70.4 us
  transfers between devices with their start and end apart: 23, of which 22 were waited for; matrix products, arithmetic and copies ran while one was open for 12% of the time, Pallas kernels for 0%

commit v1 on v0

--- a/solution.py
+++ b/solution.py
@@ -49,7 +49,11 @@
 
 
 def heads_total(partial_value):
-    return lax.psum(partial_value.astype(jnp.bfloat16), "tensor").astype(jnp.float32)
+
+    def recover_fields_here(inp):
+        return jnp.sum(lax.all_gather(inp, axis_name="tensor"), axis=0)
+
+    return recover_fields_here(partial_value.astype(jnp.bfloat16)).astype(jnp.float32)
 
 
 def inputs_total(partial_value):

time: 1280 us -> 1240 us (0.969)
  waiting for transfers between devices: 837 us -> 773 us
  other arithmetic: 105 us -> 118 us
    psum x6 -> x0, waiting for transfers between devices: 114 us -> none  [heads_total(): lax.psum(partial_value.astype(jnp.bfloat16), 'tensor').astype(jnp.float32)]
    all_gather x0 -> x6, waiting for transfers between devices: none -> 36.4 us  [recover_fields_here(): return jnp.sum(lax.all_gather(inp, axis_name='tensor'), axis=0)]
    reduce_sum x0 -> x6, other arithmetic: none -> 15.6 us  [recover_fields_here(): return jnp.sum(lax.all_gather(inp, axis_name='tensor'), axis=0)]
    psum x5 -> x6, waiting for transfers between devices: 78.4 us -> 86.6 us  [inputs_total(): lax.psum(partial_value.astype(jnp.bfloat16), 'tensor').astype(jnp.float32)]
    another operation x19 -> x18, other arithmetic: 29.5 us -> 24.9 us  [body(): stacked = jax.tree.map(lambda *entries: jnp.stack(entries), *saved)]
    unnamed x372 -> x390, local copies, waits for them, and re-layouts: 39.3 us -> 39.5 us
  transfers between devices with their start and end apart: 23 -> 24, of which waited for: 22 -> 21; matrix products, arithmetic and copies ran while one was open for 12% -> 15% of each run, Pallas kernels for 0% -> 0%
where the time goes in v1:
time: 1240 us; the launch traced here: 1230 us
  waiting for transfers between devices  773 us (62%)
  matrix products  245 us (20%)
  other arithmetic  118 us (10%)
  local copies, waits for them, and re-layouts  54.3 us (4%)
  starting transfers between devices  25.2 us (2%)
  between operations  17.2 us (1%)
    reduce_scatter x1, waiting for transfers between devices, body(): lax.psum_scatter(ffn_sums[0][None].astype(jnp.bfloat16), 'dp', scatter_di...  119 us
    reduce_scatter x1, waiting for transfers between devices, body(): lax.psum_scatter(ffn_sums[1][None].astype(jnp.bfloat16), 'dp', scatter_di...  118 us
    reduce_scatter x1, waiting for transfers between devices, body(): lax.psum_scatter(ffn_sums[2][None].astype(jnp.bfloat16), 'dp', scatter_di...  118 us
    dot_general x21, matrix products, over_rows(): lax.dot_general(left, right, (((0,), (0,)), ((), ())), preferred_element_...  102 us
    psum x6, waiting for transfers between devices, inputs_total(): lax.psum(partial_value.astype(jnp.bfloat16), 'tensor').astype(jnp.float32)  86.6 us
    ppermute x4, waiting for transfers between devices, passed_along(): return lax.ppermute(value, axis, pairs)  74.5 us
    reduce_scatter x1, waiting for transfers between devices, body(): lax.psum_scatter(attn_sums[3][None].astype(jnp.bfloat16), 'dp', scatter_d...  70.4 us
    reduce_scatter x1, waiting for transfers between devices, body(): lax.psum_scatter(attn_sums[0][None].astype(jnp.bfloat16), 'dp', scatter_d...  70.3 us
  transfers between devices with their start and end apart: 24, of which 21 were waited for; matrix products, arithmetic and copies ran while one was open for 15% of the time, Pallas kernels for 0%

profile of v1, /device:TPU:0, one launch (start us, length us, event | category | flops | bytes accessed | tf_op | source)
XLA Modules:
  0.0 1232.6 jit_solution(2559118250470027013)
XLA Ops:
  13.6 4.3 copy.78
  17.9 2.8 fusion.330
  32.4 12.6 %all-gather.13.cloned.1.call-done = bf16[512,1536]{1,0:T(8,128)(2,1)} async-done(((bf16[256,1536]{1,0:T(8,128)(2,1)}), bf16[512,1536]{1,0:T(8,128)(2,1)}) %all-gather.13.cloned.1.call-update) | async-done | bytes 1572880 | tf_op jit(solution)/shard_map/all_gather | solution.py:54
  48.7 5.0 fusion.37
  53.8 3.6 multiply_convert_fusion.2
  61.1 11.7 all-gather.17.cloned.1.call-start
  72.8 2.8 reduce_sum.292
  77.5 3.8 collective-permute-start
  81.3 17.2 %collective-permute-done = bf16[256,1536]{1,0:T(8,128)(2,1)S(1)} collective-permute-done((bf16[256,1536]{1,0:T(8,128)(2,1)S(1)}, bf16[256,1536]{1,0:T(8,128)(2,1)S(1)}, u32[]{:S(2)}, u32[]{:S(2)}) %collective-permute-start) | collective-permute-done | bytes 786464 | tf_op jit(solution)/shard_map/ppermute | solution.py:14
  112.8 11.8 all-gather.17.cloned.1.call-done
  124.6 2.8 reduce_sum.295
  130.4 5.4 fusion.35
  135.8 3.4 multiply_convert_fusion.1
  143.0 11.1 all-gather.19.cloned.1.call-done
  154.1 2.8 reduce_sum.297
  156.9 3.0 fusion.464
  159.9 4.5 collective-permute-start.1
  164.4 16.7 %collective-permute-done.1 = bf16[256,1536]{1,0:T(8,128)(2,1)} collective-permute-done((bf16[256,1536]{1,0:T(8,128)(2,1)}, bf16[256,1536]{1,0:T(8,128)(2,1)}, u32[]{:S(2)}, u32[]{:S(2)}) %collective-permute-start.1) | collective-permute-done | bytes 786464 | tf_op jit(solution)/shard_map/ppermute | solution.py:14
  197.0 4.2 multiply_convert_fusion.3
  208.6 2.8 reduce_sum.300
  214.4 5.4 fusion.33
  219.8 3.2 multiply_convert_fusion
  232.5 5.4 fusion.19
  237.9 5.7 fusion.67
  244.2 5.8 fusion.76
  250.2 5.0 pad_maximum_fusion.2
  255.2 8.9 all-reduce.7.cloned.1.call-done
  264.1 2.8 fusion.182
  290.2 2.8 reduce_sum.302
  293.0 14.0 %all-reduce.9.cloned.1.call-done = bf16[256,1536]{1,0:T(8,128)(2,1)} async-done(((bf16[256,1536]{1,0:T(8,128)(2,1)}), bf16[256,1536]{1,0:T(8,128)(2,1)}) %all-reduce.9.cloned.1.call-update) | async-done | bytes 786448 | tf_op jit(solution)/shard_map/psum | solution.py:60
  309.6 4.0 fusion.460
  315.2 20.1 %collective-permute-done.2 = bf16[256,1536]{1,0:T(8,128)(2,1)S(1)} collective-permute-done((bf16[256,1536]{1,0:T(8,128)(2,1)S(1)}, bf16[256,1536]{1,0:T(8,128)(2,1)S(1)}, u32[]{:S(2)}, u32[]{:S(2)}) %collective-permute-start.2) | collective-permute-done | bytes 786464 | tf_op jit(solution)/shard_map/ppermute | solution.py:14
  335.4 6.6 fusion.118
  346.8 3.1 fusion.112
  350.0 16.2 %all-reduce.11.cloned.1.call-done = bf16[256,1536]{1,0:T(8,128)(2,1)} async-done(((bf16[256,1536]{1,0:T(8,128)(2,1)}), bf16[256,1536]{1,0:T(8,128)(2,1)}) %all-reduce.11.cloned.1.call-update) | async-done | bytes 786448 | tf_op jit(solution)/shard_map/psum | solution.py:60
  388.1 18.7 %all-reduce.13.cloned.1.call-done = bf16[256,1536]{1,0:T(8,128)(2,1)} async-done(((bf16[256,1536]{1,0:T(8,128)(2,1)}), bf16[256,1536]{1,0:T(8,128)(2,1)}) %all-reduce.13.cloned.1.call-update) | async-done | bytes 786448 | tf_op jit(solution)/shard_map/psum | solution.py:60
  409.3 2.8 fusion.169
  413.4 20.6 %collective-permute-done.3 = bf16[256,1536]{1,0:T(8,128)(2,1)} collective-permute-done((bf16[256,1536]{1,0:T(8,128)(2,1)}, bf16[256,1536]{1,0:T(8,128)(2,1)}, u32[]{:S(2)}, u32[]{:S(2)}) %collective-permute-start.3) | collective-permute-done | bytes 786464 | tf_op jit(solution)/shard_map/ppermute | solution.py:14
  435.5 6.6 fusion.104
  442.1 5.4 fusion.15
  447.5 5.5 fusion.61
  453.3 3.2 fusion.98
  458.8 13.7 %all-reduce.15.cloned.1.call-done = bf16[256,1536]{1,0:T(8,128)(2,1)} async-done(((bf16[256,1536]{1,0:T(8,128)(2,1)}), bf16[256,1536]{1,0:T(8,128)(2,1)}) %all-reduce.15.cloned.1.call-update) | async-done | bytes 786448 | tf_op jit(solution)/shard_map/psum | solution.py:60
  496.3 3.3 fusion.42
  499.6 15.1 %all-reduce.17.cloned.1.call-done = bf16[256,1536]{1,0:T(8,128)(2,1)} async-done(((bf16[256,1536]{1,0:T(8,128)(2,1)}), bf16[256,1536]{1,0:T(8,128)(2,1)}) %all-reduce.17.cloned.1.call-update) | async-done | bytes 786448 | tf_op jit(solution)/shard_map/psum | solution.py:60
  518.3 3.6 fusion.57
  543.1 6.4 fusion.307
  549.5 6.5 fusion.303
  556.0 12.5 %fusion = bf16[1,1536,2048]{2,1,0:T(8,128)(2,1)} fusion(bf16[256,2048]{1,0:T(8,128)(2,1)S(1)} %copy-done.124, f32[1536,2048]{1,0:T(8,128)} %fusion.303, f32[1536,2048]{1,0:T(8,128)} %fusion.307, f32[]{:T(128)S(6)} %convert_element_type.703, f32[]{:T(128)S(6)} %convert_element_type.702, f32[]{:T(128)S(6)} %convert_element_type.701, ...), kind=kOutput, calls=%fused_computation.3 | convolution fusion | flops 1629487104 | bytes 33292304 | tf_op jit(solution)/shard_map/dot_general | solution.py:46
  569.7 7.7 fusion.305
  577.4 6.5 fusion.301
  583.9 12.5 %fusion.1 = bf16[1,1536,2048]{2,1,0:T(8,128)(2,1)} fusion(bf16[256,2048]{1,0:T(8,128)(2,1)S(1)} %copy-done.122, f32[1536,2048]{1,0:T(8,128)} %fusion.301, f32[1536,2048]{1,0:T(8,128)} %fusion.305, f32[]{:T(128)S(6)} %convert_element_type.703, f32[]{:T(128)S(6)} %convert_element_type.702, f32[]{:T(128)S(6)} %convert_element_type.701, ...), kind=kOutput, calls=%fused_computation.4 | convolution fusion | flops 1629487104 | bytes 33292304 | tf_op jit(solution)/shard_map/dot_general | solution.py:46
  599.7 6.4 fusion.264
  606.1 6.5 fusion.262
  612.6 12.6 %fusion.2 = bf16[1,1536,2048]{2,1,0:T(8,128)(2,1)} fusion(bf16[256,1536]{1,0:T(8,128)(2,1)S(1)} %copy-done.43, f32[1536,2048]{1,0:T(8,128)} %fusion.262, f32[1536,2048]{1,0:T(8,128)} %fusion.264, f32[]{:T(128)S(6)} %convert_element_type.703, f32[]{:T(128)S(6)} %convert_element_type.702, f32[]{:T(128)S(6)} %convert_element_type.701, ...), kind=kOutput, calls=%fused_computation.5 | convolution fusion | flops 1629487104 | bytes 33292304 | tf_op jit(solution)/shard_map/dot_general | solution.py:46
  626.3 3.3 fusion.196
  631.4 3.1 fusion.193
  636.1 13.1 %reduce-scatter.13.cloned.1.call-done = bf16[1,192,384]{2,1,0:T(8,128)(2,1)} async-done(((bf16[1,1536,384]{2,1,0:T(8,128)(2,1)}), bf16[1,192,384]{2,1,0:T(8,128)(2,1)}) %reduce-scatter.13.cloned.1.call-update) | async-done | bytes 147472 | tf_op jit(solution)/shard_map/reduce_scatter | solution.py:323
  650.9 65.5 %reduce-scatter.15.cloned.1.call-done = bf16[1,192,384]{2,1,0:T(8,128)(2,1)} async-done(((bf16[1,1536,384]{2,1,0:T(8,128)(2,1)}), bf16[1,192,384]{2,1,0:T(8,128)(2,1)}) %reduce-scatter.15.cloned.1.call-update) | async-done | bytes 147472 | tf_op jit(solution)/shard_map/reduce_scatter | solution.py:326
  718.0 70.3 %reduce-scatter.11.cloned.1.call-done = bf16[1,192,768]{2,1,0:T(8,128)(2,1)} async-done(((bf16[1,1536,768]{2,1,0:T(8,128)(2,1)}), bf16[1,192,768]{2,1,0:T(8,128)(2,1)}) %reduce-scatter.11.cloned.1.call-update) | async-done | bytes 294928 | tf_op jit(solution)/shard_map/reduce_scatter | solution.py:320
  790.1 70.4 %reduce-scatter.17.cloned.1.call-done = bf16[1,192,768]{2,1,0:T(8,128)(2,1)} async-done(((bf16[1,1536,768]{2,1,0:T(8,128)(2,1)}), bf16[1,192,768]{2,1,0:T(8,128)(2,1)}) %reduce-scatter.17.cloned.1.call-update) | async-done | bytes 294928 | tf_op jit(solution)/shard_map/reduce_scatter | solution.py:329
  862.3 118.9 %reduce-scatter.19.cloned.1.call-done = bf16[1,192,2048]{2,1,0:T(8,128)(2,1)} async-done(((bf16[1,1536,2048]{2,1,0:T(8,128)(2,1)}), bf16[1,192,2048]{2,1,0:T(8,128)(2,1)}) %reduce-scatter.19.cloned.1.call-update) | async-done | bytes 786448 | tf_op jit(solution)/shard_map/reduce_scatter | solution.py:332
  983.7 118.4 %reduce-scatter.21.cloned.1.call-done = bf16[1,192,2048]{2,1,0:T(8,128)(2,1)} async-done(((bf16[1,1536,2048]{2,1,0:T(8,128)(2,1)}), bf16[1,192,2048]{2,1,0:T(8,128)(2,1)}) %reduce-scatter.21.cloned.1.call-update) | async-done | bytes 786448 | tf_op jit(solution)/shard_map/reduce_scatter | solution.py:335
  1104.6 118.3 %reduce-scatter.23.cloned.1.call-done = bf16[1,192,2048]{2,1,0:T(8,128)(2,1)} async-done(((bf16[1,1536,2048]{2,1,0:T(8,128)(2,1)}), bf16[1,192,2048]{2,1,0:T(8,128)(2,1)}) %reduce-scatter.23.cloned.1.call-update) | async-done | bytes 786448 | tf_op jit(solution)/shard_map/reduce_scatter | solution.py:338
  (613 shorter events, 216.7 us)
Async XLA Ops:
  7.2 23.4 %copy-start = (bf16[1,1536,768]{2,1,0:T(8,128)(2,1)S(1)}, bf16[1,1536,768]{2,1,0:T(8,128)(2,1)}, u32[]{:S(2)}) copy-start(bf16[1,1536,768]{2,1,0:T(8,128)(2,1)} %param.16) | copy-start | bytes 7077892
  7.2 37.8 %all-gather.13.cloned.1.call-start = ((), (), s32[]{:S(2)}) async-start(), calls=%async_computation.21 | async-start | bytes 2359296 | tf_op jit(solution)/shard_map/all_gather | solution.py:54
  10.7 7.3 copy-start.163
  27.3 353.1 %copy-start.26 = (f32[256,96]{0,1:T(8,128)}, f32[256,96]{0,1:T(8,128)S(1)}, u32[]{:S(2)}) copy-start(f32[256,96]{0,1:T(8,128)S(1)} %get-tuple-element.110) | copy-start | bytes 294916
  27.3 353.3 %copy-start.23 = (f32[256,96]{0,1:T(8,128)}, f32[256,96]{0,1:T(8,128)S(1)}, u32[]{:S(2)}) copy-start(f32[256,96]{0,1:T(8,128)S(1)} %get-tuple-element.109) | copy-start | bytes 294916
  32.4 40.5 %all-gather.15.cloned.1.call-start = ((), (), s32[]{:S(2)}) async-start(), calls=%async_computation.22 | async-start | bytes 2359296 | tf_op jit(solution)/shard_map/all_gather | solution.py:54
  46.7 28.8 %copy-start.28 = (bf16[256,1536]{1,0:T(8,128)(2,1)}, bf16[256,1536]{1,0:T(8,128)(2,1)S(1)}, u32[]{:S(2)}) copy-start(bf16[256,1536]{1,0:T(8,128)(2,1)S(1)} %reduce_sum.290) | copy-start | bytes 2359300
  46.8 6.9 slice-start.6
  48.7 9.6 slice-start
  61.1 63.6 %all-gather.17.cloned.1.call-start = ((), (), s32[]{:S(2)}) async-start(), calls=%async_computation.23 | async-start | bytes 2359296 | tf_op jit(solution)/shard_map/all_gather | solution.py:54
  75.6 22.9 %copy-start.19 = (bf16[2,1,256,1536]{3,2,1,0:T(8,128)(2,1)S(1)}, bf16[2,1,256,1536]{3,2,1,0:T(8,128)(2,1)}, u32[]{:S(2)}) copy-start(bf16[2,1,256,1536]{3,2,1,0:T(8,128)(2,1)} %param.10) | copy-start | bytes 4718596
  75.6 23.3 %copy-start.31 = (bf16[1,1536,384]{2,1,0:T(8,128)(2,1)S(1)}, bf16[1,1536,384]{2,1,0:T(8,128)(2,1)}, u32[]{:S(2)}) copy-start(bf16[1,1536,384]{2,1,0:T(8,128)(2,1)} %param.15) | copy-start | bytes 3538948
  77.4 22.7 %copy-start.81 = (bf16[1,1536,768]{1,2,0:T(8,128)(2,1)S(1)}, bf16[1,1536,768]{1,2,0:T(8,128)(2,1)}, u32[]{:S(2)}) copy-start(bf16[1,1536,768]{1,2,0:T(8,128)(2,1)} %copy.78) | copy-start | bytes 7077892
  77.5 21.0 %collective-permute-start = (bf16[256,1536]{1,0:T(8,128)(2,1)S(1)}, bf16[256,1536]{1,0:T(8,128)(2,1)S(1)}, u32[]{:S(2)}, u32[]{:S(2)}) collective-permute-start(bf16[256,1536]{1,0:T(8,128)(2,1)S(1)} %fusion.189), channel_id=1, source_target_pairs={{0,16},{1,17},{2,18},{3,19},{4,20},{5,21},{6,22},{7,23},{8,24},{9,... | collective-permute-start | bytes 2359304 | tf_op jit(solution)/shard_map/ppermute | solution.py:14
  98.8 58.1 %copy-start.16 = (bf16[256,1536]{1,0:T(8,128)(2,1)}, bf16[256,1536]{1,0:T(8,128)(2,1)S(1)}, u32[]{:S(2)}) copy-start(bf16[256,1536]{1,0:T(8,128)(2,1)S(1)} %get-tuple-element.27) | copy-start | bytes 2359300
  112.7 41.4 %all-gather.19.cloned.1.call-start = ((), (), s32[]{:S(2)}) async-start(), calls=%async_computation.24 | async-start | bytes 2359296 | tf_op jit(solution)/shard_map/all_gather | solution.py:54
  128.9 6.8 slice-start.8
  130.4 9.9 slice-start.2
  143.0 65.6 %all-gather.21.cloned.1.call-start = ((), (), s32[]{:S(2)}) async-start(), calls=%async_computation.25 | async-start | bytes 2359296 | tf_op jit(solution)/shard_map/all_gather | solution.py:54
  159.9 21.2 %collective-permute-start.1 = (bf16[256,1536]{1,0:T(8,128)(2,1)}, bf16[256,1536]{1,0:T(8,128)(2,1)}, u32[]{:S(2)}, u32[]{:S(2)}) collective-permute-start(bf16[256,1536]{1,0:T(8,128)(2,1)} %get-tuple-element.46), channel_id=1, source_target_pairs={{0,16},{1,17},{2,18},{3,19},{4,20},{5,21},{6,22},{7,23},{8,24},{9,... | collective-permute-start | bytes 2359304 | tf_op jit(solution)/shard_map/ppermute | solution.py:14
  164.4 18.2 %copy-start.32 = (bf16[1,1536,384]{2,1,0:T(8,128)(2,1)S(1)}, bf16[1,1536,384]{2,1,0:T(8,128)(2,1)}, u32[]{:S(2)}) copy-start(bf16[1,1536,384]{2,1,0:T(8,128)(2,1)} %param.15) | copy-start | bytes 3538948
  164.4 19.5 %copy-start.82 = (bf16[1,1536,768]{1,2,0:T(8,128)(2,1)S(1)}, bf16[1,1536,768]{1,2,0:T(8,128)(2,1)}, u32[]{:S(2)}) copy-start(bf16[1,1536,768]{1,2,0:T(8,128)(2,1)} %copy.78) | copy-start | bytes 7077892
  196.4 67.7 %all-reduce.7.cloned.1.call-start = ((), (), s32[]{:S(2)}) async-start(), calls=%async_computation.8 | async-start | bytes 1572864 | tf_op jit(solution)/shard_map/psum | solution.py:60
  212.9 6.8 slice-start.10
  223.0 5.7 slice-start.4
  223.8 5.7 slice-start.5
  237.8 5.8 copy-start.168
  237.9 5.8 copy-start.172
  243.6 46.7 %all-gather.23.cloned.1.call-start = ((), (), s32[]{:S(2)}) async-start(), calls=%async_computation.26 | async-start | bytes 2359296 | tf_op jit(solution)/shard_map/all_gather | solution.py:54
  250.1 56.9 %all-reduce.9.cloned.1.call-start = ((), (), s32[]{:S(2)}) async-start(), calls=%async_computation.9 | async-start | bytes 1572864 | tf_op jit(solution)/shard_map/psum | solution.py:60
  286.6 79.6 %all-reduce.11.cloned.1.call-start = ((), (), s32[]{:S(2)}) async-start(), calls=%async_computation.10 | async-start | bytes 1572864 | tf_op jit(solution)/shard_map/psum | solution.py:60
  309.5 25.7 %copy-start.46 = (bf16[2,1,256,1536]{3,2,1,0:T(8,128)(2,1)S(1)}, bf16[2,1,256,1536]{3,2,1,0:T(8,128)(2,1)}, u32[]{:S(2)}) copy-start(bf16[2,1,256,1536]{3,2,1,0:T(8,128)(2,1)} %param.11) | copy-start | bytes 4718596
  309.5 32.5 %slice-start.12 = ((s8[6291456]{0:T(1024)(128)(4,1)}), s8[4194304]{0:T(1024)(128)(4,1)S(1)}, s32[]{:S(2)}) async-start(s8[6291456]{0:T(1024)(128)(4,1)} %bitcast.962), calls=%async_computation.40 | async-start | bytes 8388608
  309.6 34.4 %slice-start.14 = ((s8[6291456]{0:T(1024)(128)(4,1)}), s8[4194304]{0:T(1024)(128)(4,1)S(1)}, s32[]{:S(2)}) async-start(s8[6291456]{0:T(1024)(128)(4,1)} %bitcast.964), calls=%async_computation.42 | async-start | bytes 8388608
  313.6 28.5 %copy-start.69 = (bf16[256,1536]{1,0:T(8,128)(2,1)}, bf16[256,1536]{1,0:T(8,128)(2,1)S(1)}, u32[]{:S(2)}) copy-start(bf16[256,1536]{1,0:T(8,128)(2,1)S(1)} %get-tuple-element.76) | copy-start | bytes 2359300
  313.6 21.7 %collective-permute-start.2 = (bf16[256,1536]{1,0:T(8,128)(2,1)S(1)}, bf16[256,1536]{1,0:T(8,128)(2,1)S(1)}, u32[]{:S(2)}, u32[]{:S(2)}) collective-permute-start(bf16[256,1536]{1,0:T(8,128)(2,1)S(1)} %get-tuple-element.76), channel_id=1, source_target_pairs={{16,0},{17,1},{18,2},{19,3},{20,4},{21,5},{22,6},{23,7},{24,8},{25... | collective-permute-start | bytes 2359304 | tf_op jit(solution)/shard_map/ppermute | solution.py:14
  335.4 33.6 %copy-start.39 = (bf16[256,1536]{1,0:T(8,128)(2,1)}, bf16[256,1536]{1,0:T(8,128)(2,1)S(1)}, u32[]{:S(2)}) copy-start(bf16[256,1536]{1,0:T(8,128)(2,1)S(1)} %bitcast_select_fusion.1) | copy-start | bytes 2359300
  335.4 6.7 slice-start.13
  335.4 8.6 slice-start.15
  346.7 60.0 %all-reduce.13.cloned.1.call-start = ((), (), s32[]{:S(2)}) async-start(), calls=%async_computation.11 | async-start | bytes 1572864 | tf_op jit(solution)/shard_map/psum | solution.py:60
  386.4 86.1 %all-reduce.15.cloned.1.call-start = ((), (), s32[]{:S(2)}) async-start(), calls=%async_computation.12 | async-start | bytes 1572864 | tf_op jit(solution)/shard_map/psum | solution.py:60
  412.1 21.9 %collective-permute-start.3 = (bf16[256,1536]{1,0:T(8,128)(2,1)}, bf16[256,1536]{1,0:T(8,128)(2,1)}, u32[]{:S(2)}, u32[]{:S(2)}) collective-permute-start(bf16[256,1536]{1,0:T(8,128)(2,1)} %fusion.169), channel_id=1, source_target_pairs={{16,0},{17,1},{18,2},{19,3},{20,4},{21,5},{22,6},{23,7},{24,8},{25... | collective-permute-start | bytes 2359304 | tf_op jit(solution)/shard_map/ppermute | solution.py:14
  435.5 6.6 copy-start.41
  453.0 61.7 %all-reduce.17.cloned.1.call-start = ((), (), s32[]{:S(2)}) async-start(), calls=%async_computation.13 | async-start | bytes 1572864 | tf_op jit(solution)/shard_map/psum | solution.py:60
  494.4 140.1 %reduce-scatter.25.cloned.1.call-start = ((), (), s32[]{:S(2)}) async-start(), calls=%async_computation.27 | async-start | bytes 442368
  496.3 18.5 %copy-start.162 = (f32[1,256,1]{1,2,0:T(1,128)S(1)}, f32[1,256,1]{1,2,0:T(1,128)}, u32[]{:S(2)}) copy-start(f32[1,256,1]{1,2,0:T(1,128)} %get-tuple-element.83) | copy-start | bytes 3076
  496.3 20.3 %copy-start.152 = (f32[1536]{0:T(1024)S(1)}, f32[1536]{0:T(1024)}, u32[]{:S(2)}) copy-start(f32[1536]{0:T(1024)} %get-tuple-element.16) | copy-start | bytes 18436
  496.3 20.3 %copy-start.154 = (f32[1536]{0:T(1024)S(1)}, f32[1536]{0:T(1024)}, u32[]{:S(2)}) copy-start(f32[1536]{0:T(1024)} %get-tuple-element.18) | copy-start | bytes 18436
  499.6 18.7 %copy-start.92 = (bf16[256,4,96]{0,2,1:T(8,128)(2,1)S(1)}, bf16[256,4,96]{0,2,1:T(8,128)(2,1)}, u32[]{:S(2)}) copy-start(bf16[256,4,96]{0,2,1:T(8,128)(2,1)} %copy-done.91) | copy-start | bytes 589828
  518.2 131.0 %reduce-scatter.13.cloned.1.call-start = ((), (), s32[]{:S(2)}) async-start(), calls=%async_computation.15 | async-start | bytes 1327104 | tf_op jit(solution)/shard_map/reduce_scatter | solution.py:323
  521.9 194.4 %reduce-scatter.15.cloned.1.call-start = ((), (), s32[]{:S(2)}) async-start(), calls=%async_computation.16 | async-start | bytes 1327104 | tf_op jit(solution)/shard_map/reduce_scatter | solution.py:326
  526.5 261.8 %reduce-scatter.11.cloned.1.call-start = ((), (), s32[]{:S(2)}) async-start(), calls=%async_computation.14 | async-start | bytes 2654208 | tf_op jit(solution)/shard_map/reduce_scatter | solution.py:320
  532.6 327.9 %reduce-scatter.17.cloned.1.call-start = ((), (), s32[]{:S(2)}) async-start(), calls=%async_computation.17 | async-start | bytes 2654208 | tf_op jit(solution)/shard_map/reduce_scatter | solution.py:329
  540.2 441.1 %reduce-scatter.19.cloned.1.call-start = ((), (), s32[]{:S(2)}) async-start(), calls=%async_computation.18 | async-start | bytes 7077888 | tf_op jit(solution)/shard_map/reduce_scatter | solution.py:332
  543.0 12.9 %copy-start.14 = (bf16[3,256,1536]{2,1,0:T(8,128)(2,1)}, bf16[3,256,1536]{2,1,0:T(8,128)(2,1)S(1)}, u32[]{:S(2)}) copy-start(bf16[3,256,1536]{2,1,0:T(8,128)(2,1)S(1)} %pad_maximum_fusion.6) | copy-start | bytes 7077892
  543.1 6.4 copy-start.120
  549.5 6.5 copy-start.124
  568.5 533.6 %reduce-scatter.21.cloned.1.call-start = ((), (), s32[]{:S(2)}) async-start(), calls=%async_computation.19 | async-start | bytes 7077888 | tf_op jit(solution)/shard_map/reduce_scatter | solution.py:335
  569.7 7.7 copy-start.15
  569.7 7.7 copy-start.118
  577.4 6.5 copy-start.122
  596.4 626.5 %reduce-scatter.23.cloned.1.call-start = ((), (), s32[]{:S(2)}) async-start(), calls=%async_computation.20 | async-start | bytes 7077888 | tf_op jit(solution)/shard_map/reduce_scatter | solution.py:338
  599.7 6.4 copy-start.40
  606.1 6.5 copy-start.43
  (152 other events, 388.2 us)
Sparse Core Ops, SparseCore 0:
  32.5 12.5 all-gather.12
  61.2 10.9 all-gather.14
  112.9 11.7 all-gather.16
  143.1 10.9 all-gather.18
  196.6 11.9 all-gather.20
  243.7 20.3 all-reduce.6
  265.7 10.9 all-gather.22
  286.7 20.2 all-reduce.8
  346.9 19.2 all-reduce.10
  386.5 20.1 all-reduce.12
  453.2 19.2 all-reduce.14
  494.6 20.1 all-reduce.16
  518.6 63.3 reduce-scatter.24
  585.2 63.9 reduce-scatter.12
  652.4 63.8 reduce-scatter.14
  719.7 68.5 reduce-scatter.10
  791.6 68.8 reduce-scatter.16
  864.0 117.2 reduce-scatter.18
  984.8 117.2 reduce-scatter.20
  1105.6 117.2 reduce-scatter.22
